TPU v7x, 32 devices: a whole 2x2x4 slice. The times are simulated.
32 devices in a mesh: grp: 2 (over y), exp: 4 (over z), tp: 4 (over x, core).
Axes of the slice: x: 2, y: 2, z: 4, core: 2. Of those that a mesh axis runs over, the one named last changes fastest.
Arguments:
- tokens: bfloat16 [128, 3584], P(('grp', 'exp'), 'tp'), parts along dimension 0, may hold values from -6 to 6
- gate_up_weight: bfloat16 [3584, 2, 18944], P('tp', None, 'exp'), may hold values from -0.09375 to 0.09375
- down_weight: bfloat16 [18944, 3584], P('exp', 'tp'), may hold values from -0.046875 to 0.046875
- adapter_in: bfloat16 [4, 3584, 16], P('exp', 'tp'), may hold values from -0.09375 to 0.09375
- adapter_out: bfloat16 [4, 16, 3584], P('exp', None, 'tp'), may hold values from -1.5 to 1.5
- expert_ids: int32 [128, 2], P(('grp', 'exp')), parts along dimension 0, may hold values from 0 to 3, all different within a row; in each aligned block of 16 rows (0 to 15, 16 to 31, ...) at most 16 rows name the same one
- route_weight: float32 [128, 2], P(('grp', 'exp')), parts along dimension 0, may hold values from 0.2 to 1
Outputs:
- mixed: bfloat16 [128, 3584], P(('grp', 'exp'), 'tp'), parts along dimension 0
There are 2 independent parts, one for each index of `grp`. A program takes and returns all parts, laid end to end along the dimension named above; an argument that names none is the same for every part. Nothing has to cross between parts.
Inputs may be any that keep to these rules, and one draw needn't show every extreme that they name: `expert_ids`: each row names 2 different experts. Among the 16 rows of one index of exp (aligned blocks of 16 rows) no expert is named by more than 16 rows, and in every draw some expert is named by exactly 16 rows of some block.
All inputs are finite; a program needn't handle non-finite values.
Results may differ from a plain program's by a relative error of at most 0.025.
Values may be sent and summed in bfloat16 or wider, within the bound.
A program may use at most 64 MiB of HBM per device.

v0:
```python
import jax
import jax.numpy as jnp
from jax import lax
from jax.sharding import PartitionSpec as P


def local(tokens, gate_up_weight, down_weight, adapter_in, adapter_out, expert_ids, route_weight):
    exp_count = lax.axis_size("exp")
    own_rows, feat_width = tokens.shape
    all_tokens = lax.all_gather(tokens, "exp", axis=0, tiled=True)
    hidden_width = gate_up_weight.shape[2]
    pair_weight = gate_up_weight.reshape(feat_width, 2 * hidden_width)
    pair_share = lax.psum_scatter(
        jnp.dot(all_tokens, pair_weight, preferred_element_type=jnp.float32).astype(jnp.bfloat16),
        "tp",
        scatter_dimension=0,
        tiled=True,
    ).astype(jnp.float32)
    hidden_share = (
        jax.nn.silu(pair_share[:, :hidden_width]) * pair_share[:, hidden_width:]
    ).astype(jnp.bfloat16)
    hidden = lax.all_gather(hidden_share, "tp", axis=0, tiled=True)
    base_out = lax.psum_scatter(
        jnp.dot(hidden, down_weight, preferred_element_type=jnp.float32).astype(jnp.bfloat16),
        "exp",
        scatter_dimension=0,
        tiled=True,
    ).astype(jnp.float32)
    top_count = expert_ids.shape[1]
    expert_count = adapter_in.shape[0] * exp_count
    flat_ids = expert_ids.reshape(own_rows * top_count)
    flat_weight = route_weight.reshape(own_rows * top_count)
    expert_hits = (flat_ids[:, None] == jnp.arange(expert_count, dtype=jnp.int32)[None, :]).astype(
        jnp.int32
    )
    capacity = max(2, 2 * top_count * own_rows // expert_count)
    slot_index = jnp.sum((jnp.cumsum(expert_hits, axis=0) - expert_hits) * expert_hits, axis=1)
    slot_target = flat_ids * capacity + slot_index
    slot_hits = (
        slot_target[:, None] == jnp.arange(expert_count * capacity, dtype=jnp.int32)[None, :]
    )
    combine_matrix = jnp.sum(
        (slot_hits.astype(jnp.float32) * flat_weight[:, None]).reshape(
            own_rows, top_count, expert_count * capacity
        ),
        axis=1,
    )
    dispatch_matrix = slot_hits.T.astype(jnp.bfloat16)
    repeated = jnp.repeat(tokens, top_count, axis=0)
    outgoing = jnp.dot(dispatch_matrix, repeated, preferred_element_type=jnp.float32).astype(
        jnp.bfloat16
    )
    outgoing = outgoing.reshape(expert_count, capacity, feat_width)
    rank_partial = jnp.einsum(
        "scd,dr->scr",
        lax.all_to_all(outgoing, "exp", split_axis=0, concat_axis=0, tiled=True),
        adapter_in[0],
        preferred_element_type=jnp.float32,
    )
    rank_mid = lax.psum(rank_partial, "tp").astype(jnp.bfloat16)
    expert_out = jnp.einsum(
        "scr,rd->scd", rank_mid, adapter_out[0], preferred_element_type=jnp.float32
    ).astype(jnp.bfloat16)
    returned = lax.all_to_all(expert_out, "exp", split_axis=0, concat_axis=0, tiled=True)
    adapter_sum = jnp.dot(
        combine_matrix,
        returned.reshape(expert_count * capacity, feat_width).astype(jnp.float32),
        precision=lax.Precision.HIGHEST,
        preferred_element_type=jnp.float32,
    )
    return (base_out + adapter_sum).astype(jnp.bfloat16)


def solution(mesh):
    in_specs = (
        P(("grp", "exp"), "tp"),
        P("tp", None, "exp"),
        P("exp", "tp"),
        P("exp", "tp", None),
        P("exp", None, "tp"),
        P(("grp", "exp"), None),
        P(("grp", "exp"), None),
    )
    out_specs = P(("grp", "exp"), "tp")
    return jax.shard_map(local, mesh=mesh, in_specs=in_specs, out_specs=out_specs, check_vma=False)
```

profile of v0, /device:TPU:0, one launch (start us, length us, event | category | flops | bytes accessed | tf_op | source)
XLA Modules:
  0.0 105.8 jit_solution(269650311221717586)
XLA Ops:
  6.5 0.0 copy-start
  6.5 0.0 reduce-scatter.3.cloned.1.call-start
  6.5 15.4 %all_gather.6 = bf16[64,896]{1,0:T(8,128)(2,1)S(1)} all-gather(bf16[16,896]{1,0:T(8,128)(2,1)} %param.7), channel_id=1, replica_groups=mesh['grp'=2,'exp'=4,'tp'=4] {'exp'}, dimensions={0}, use_global_device_ids=true | all-gather | bytes 143360 | tf_op jit(solution)/shard_map/all_gather | solution.py:10
  22.0 9.7 %copy.22 = bf16[112,8,2,4736]{3,1,2,0:T(8,128)(2,1)S(1)} copy(bf16[112,8,2,4736]{3,2,1,0:T(2,128)(2,1)} %bitcast.22) | data formatting | bytes 33947648
  31.7 0.0 copy-start.3
  31.7 0.0 copy-start.1
  31.7 0.0 copy-start.2
  31.7 3.5 %convolution_convert_fusion = bf16[64,9472]{1,0:T(8,128)(2,1)} fusion(bf16[64,896]{1,0:T(8,128)(2,1)S(1)} %all_gather.6, bf16[896,9472]{1,0:T(8,128)(2,1)S(1)} %bitcast.21), kind=kOutput, calls=%fused_computation | convolution fusion | flops 1086930944 | bytes 18300928 | tf_op jit(solution)/shard_map/dot_general | solution.py:14
  35.2 0.0 reduce-scatter.3.cloned.1.call-update
  35.2 0.0 copy-done.3
  35.2 0.1 copy.20
  35.3 0.1 eq.35
  35.4 0.0 copy-done.1
  35.5 0.1 fusion.6
  35.5 0.1 reduce_window_sum.11
  35.6 0.2 select_reduce_fusion.1
  35.8 1.0 convolution_convert_fusion.2
  36.8 4.8 %all-to-all-start = ((bf16[4,16,896]{2,1,0:T(8,128)(2,1)}), bf16[4,16,896]{2,1,0:T(8,128)(2,1)S(1)}, u32[]{:S(2)}, u32[]{:S(2)}) async-start(bf16[4,16,896]{2,1,0:T(8,128)(2,1)} %bitcast), calls=%async_computation.2 | async-start | bytes 229376 | tf_op jit(solution)/shard_map/all_to_all | solution.py:56
  41.6 0.1 reduce_sum.21
  41.6 0.1 copy.21
  41.7 5.7 %all-to-all-done = bf16[4,16,896]{2,1,0:T(8,128)(2,1)S(1)} async-done(((bf16[4,16,896]{2,1,0:T(8,128)(2,1)}), bf16[4,16,896]{2,1,0:T(8,128)(2,1)S(1)}, u32[]{:S(2)}, u32[]{:S(2)}) %all-to-all-start) | async-done | bytes 114720 | tf_op jit(solution)/shard_map/all_to_all | solution.py:56
  47.4 0.0 copy-done.2
  47.4 0.2 fusion.3
  47.6 11.2 %psum.7 = bf16[4,16,16]{2,1,0:T(8,128)(2,1)S(1)} all-reduce(f32[4,16,16]{2,1,0:T(8,128)S(1)} %fusion.3), channel_id=1, replica_groups=mesh['grp'=2,'exp'=4,'tp'=4] {'tp'}, use_global_device_ids=true, to_apply=%region_5.6 | all-reduce | flops 1024 | bytes 6144 | tf_op jit(solution)/shard_map/psum | solution.py:60
  58.8 0.0 copy-done
  58.8 0.8 convolution_convert_fusion.1
  59.6 3.3 %all-to-all-start.1 = ((bf16[4,16,896]{2,1,0:T(8,128)(2,1)}), bf16[4,16,896]{2,1,0:T(8,128)(2,1)S(1)}, u32[]{:S(2)}, u32[]{:S(2)}) async-start(bf16[4,16,896]{2,1,0:T(8,128)(2,1)} %convolution_convert_fusion.1), calls=%async_computation.3 | async-start | bytes 229376 | tf_op jit(solution)/shard_map/all_to_all | solution.py:64
  62.9 0.0 reduce-scatter.5.cloned.1.call-start
  63.0 0.0 reduce-scatter.3.cloned.1.call-done
  63.0 1.0 convert_element_type.34
  64.0 0.1 fusion.1
  64.1 7.7 %all_gather.7 = bf16[64,4736]{1,0:T(8,128)(2,1)S(1)} all-gather(bf16[16,4736]{1,0:T(8,128)(2,1)S(1)} %fusion.1), channel_id=1, replica_groups=mesh['grp'=2,'exp'=4,'tp'=4] {'tp'}, dimensions={0}, use_global_device_ids=true | all-gather | bytes 757760 | tf_op jit(solution)/shard_map/all_gather | solution.py:22
  71.8 0.0 copy-start.4
  71.8 5.5 %convolution_convert_fusion.3 = bf16[64,896]{1,0:T(8,128)(2,1)} fusion(bf16[64,4736]{1,0:T(8,128)(2,1)S(1)} %all_gather.7, bf16[4736,896]{1,0:T(8,128)(2,1)} %param.9), kind=kOutput, calls=%fused_computation.3 | convolution fusion | flops 543219712 | bytes 9207808 | tf_op jit(solution)/shard_map/dot_general | solution.py:24
  77.3 0.0 reduce-scatter.5.cloned.1.call-update
  77.3 0.0 copy-done.4
  77.3 0.1 select_reduce_fusion
  77.4 0.0 all-to-all-done.1
  77.4 20.0 %reduce-scatter.5.cloned.1.call-done = bf16[16,896]{1,0:T(8,128)(2,1)} async-done(((bf16[64,896]{1,0:T(8,128)(2,1)}), bf16[16,896]{1,0:T(8,128)(2,1)}) %reduce-scatter.5.cloned.1.call-update) | async-done | bytes 28688 | tf_op jit(solution)/shard_map/reduce_scatter | solution.py:23
  97.4 1.5 %fusion = bf16[16,896]{1,0:T(8,128)(2,1)} fusion(f32[16,64]{1,0:T(8,128)S(1)} %select_reduce_fusion, bf16[64,896]{1,0:T(8,128)(2,1)S(1)} %bitcast.23, bf16[16,896]{1,0:T(8,128)(2,1)} %reduce-scatter.5.cloned.1.call-done), kind=kOutput, calls=%fused_computation.5 | convolution fusion | flops 11053056 | bytes 176128 | tf_op jit(solution)/shard_map/dot_general | solution.py:65
  (4 shorter events, 0.1 us)
Async XLA Ops:
  6.5 52.3 %copy-start = (bf16[1,16,896]{2,1,0:T(8,128)(2,1)S(1)}, bf16[1,16,896]{2,1,0:T(8,128)(2,1)}, u32[]{:S(2)}) copy-start(bf16[1,16,896]{2,1,0:T(8,128)(2,1)} %param.11) | copy-start | bytes 86020
  6.5 56.4 %reduce-scatter.3.cloned.1.call-start = ((), (), s32[]{:S(2)}) async-start(), calls=%async_computation.4 | async-start | bytes 1515520 | tf_op jit(solution)/shard_map/reduce_scatter | solution.py:13
  31.7 3.5 %copy-start.3 = (s32[16,2]{0,1:T(2,128)S(1)}, s32[16,2]{0,1:T(2,128)}, u32[]{:S(2)}) copy-start(s32[16,2]{0,1:T(2,128)} %param.12) | copy-start | bytes 388
  31.7 3.7 %copy-start.1 = (bf16[16,896]{1,0:T(8,128)(2,1)S(1)}, bf16[16,896]{1,0:T(8,128)(2,1)}, u32[]{:S(2)}) copy-start(bf16[16,896]{1,0:T(8,128)(2,1)} %param.7) | copy-start | bytes 86020
  31.7 15.7 %copy-start.2 = (bf16[1,896,16]{1,2,0:T(8,128)(2,1)S(1)}, bf16[1,896,16]{1,2,0:T(8,128)(2,1)}, u32[]{:S(2)}) copy-start(bf16[1,896,16]{1,2,0:T(8,128)(2,1)} %param.10) | copy-start | bytes 86020
  36.8 10.7 %all-to-all-start = ((bf16[4,16,896]{2,1,0:T(8,128)(2,1)}), bf16[4,16,896]{2,1,0:T(8,128)(2,1)S(1)}, u32[]{:S(2)}, u32[]{:S(2)}) async-start(bf16[4,16,896]{2,1,0:T(8,128)(2,1)} %bitcast), calls=%async_computation.2 | async-start | bytes 229376 | tf_op jit(solution)/shard_map/all_to_all | solution.py:56
  59.6 17.8 %all-to-all-start.1 = ((bf16[4,16,896]{2,1,0:T(8,128)(2,1)}), bf16[4,16,896]{2,1,0:T(8,128)(2,1)S(1)}, u32[]{:S(2)}, u32[]{:S(2)}) async-start(bf16[4,16,896]{2,1,0:T(8,128)(2,1)} %convolution_convert_fusion.1), calls=%async_computation.3 | async-start | bytes 229376 | tf_op jit(solution)/shard_map/all_to_all | solution.py:64
  62.9 34.5 %reduce-scatter.5.cloned.1.call-start = ((), (), s32[]{:S(2)}) async-start(), calls=%async_computation.5 | async-start | bytes 143360 | tf_op jit(solution)/shard_map/reduce_scatter | solution.py:23
  71.8 5.5 %copy-start.4 = (f32[16,2]{0,1:T(2,128)S(1)}, f32[16,2]{0,1:T(2,128)}, u32[]{:S(2)}) copy-start(f32[16,2]{0,1:T(2,128)} %param.13) | copy-start | bytes 388
Sparse Core Ops, SparseCore 0:
  35.3 27.2 reduce-scatter.2
  77.4 19.9 reduce-scatter.4
where the time goes:
time: 106 us
  blocking collectives  34.4 us (32%)
  waiting for transfers between devices  25.7 us (24%)
  between operations  13.5 us (13%)
  matrix products  12.4 us (12%)
  local copies, waits for them, and re-layouts  10.1 us (10%)
  starting transfers between devices  8.16 us (8%)
  other arithmetic  1.49 us (1%)
    reduce_scatter x1, waiting for transfers between devices, local(): lax.psum_scatter(jnp.dot(hidden, down_weight, preferred_element_type=jnp....  20 us
    all_gather x1, blocking collectives, local(): all_tokens = lax.all_gather(tokens, 'exp', axis=0, tiled=True)  15.4 us
    psum x1, blocking collectives, local(): rank_mid = lax.psum(rank_partial, 'tp').astype(jnp.bfloat16)  11.2 us
    unnamed x12, local copies, waits for them, and re-layouts  9.81 us
    all_gather x1, blocking collectives, local(): hidden = lax.all_gather(hidden_share, 'tp', axis=0, tiled=True)  7.73 us
    all_to_all x1, waiting for transfers between devices, local(): lax.all_to_all(outgoing, 'exp', split_axis=0, concat_axis=0, tiled=True)  5.71 us
    dot_general x1, matrix products, local(): jnp.dot(hidden, down_weight, preferred_element_type=jnp.float32)  5.47 us
    all_to_all x1, starting transfers between devices, local(): lax.all_to_all(outgoing, 'exp', split_axis=0, concat_axis=0, tiled=True)  4.8 us
  transfers between devices with their start and end apart: 4, of which 2 were waited for; matrix products, arithmetic and copies ran while one was open for 9% of the time, Pallas kernels for 0%

commit v1 on v0

--- a/solution.py
+++ b/solution.py
@@ -1,10 +1,337 @@
+import functools
 import jax
 import jax.numpy as jnp
 from jax import lax
+from jax.experimental import pallas as pl
+from jax.experimental.pallas import tpu as pltpu
 from jax.sharding import PartitionSpec as P
 
-
-def local(tokens, gate_up_weight, down_weight, adapter_in, adapter_out, expert_ids, route_weight):
+LANES = 128
+CHUNK_TILES = 8
+MESH = pl.DeviceIdType.MESH
+BF16, F32 = jnp.bfloat16, jnp.float32
+
+
+def chunks_of(tiles):
+    spans, first = [], 0
+    while first < tiles:
+        count = min(CHUNK_TILES, tiles - first)
+        spans.append((first, count))
+        first += count
+    return spans
+
+
+def kernel(
+    exp_count, tok_ref, gu_ref, down_ref, ain_ref, aout_ref, ids_ref, weight_ref, out_ref,
+    gu, down, tok_all, coef_all, coef_own, lhs, ain_pad, aout_pad,
+    keep1, send1, recv1, keep2, send2, recv2, hid, total, send_f, recv_f,
+    gu_sem, down_sem, tok_send, tok_recv, coef_send, coef_recv,
+    s1_send, s1_recv, s2_send, s2_recv, hp_send, hp_recv, hx_send, hx_recv, hr_send, hr_recv,
+    f_send, f_recv,
+):
+    me = lax.axis_index("exp")
+    tp = lax.axis_index("tp")
+    own_rows, feat = tok_ref.shape
+    hidden = gu_ref.shape[2]
+    rank = ain_ref.shape[2]
+    tiles = hidden // LANES
+    spans = chunks_of(tiles)
+    last = len(spans) - 1
+    core, side = tp % 2, tp // 2
+    partner = side * 2 + (1 - core)
+    across = (1 - side) * 2 + core
+    blocks = [
+        core * 2 + side,
+        core * 2 + (1 - side),
+        (1 - core) * 2 + side,
+        (1 - core) * 2 + (1 - side),
+    ]
+    mine, crossed = blocks[0], blocks[1]
+
+    def gu_copy(t):
+        cols = pl.ds(pl.multiple_of(t * LANES, LANES), LANES)
+        return pltpu.make_async_copy(gu_ref.at[:, :, cols], gu.at[t], gu_sem.at[t])
+
+    def down_copy(j):
+        first, count = spans[j]
+        rows = pl.ds(first * LANES, count * LANES)
+        return pltpu.make_async_copy(down_ref.at[rows], down.at[rows], down_sem.at[j])
+
+    def start_gu(t, carry):
+        gu_copy(t).start()
+        return carry
+
+    lax.fori_loop(0, tiles, start_gu, 0)
+    for j in range(len(spans)):
+        down_copy(j).start()
+
+    barrier = pltpu.get_barrier_semaphore()
+    for d in range(1, exp_count):
+        pl.semaphore_signal(
+            barrier, inc=1, device_id={"exp": (me + d) % exp_count}, device_id_type=MESH
+        )
+    for peer in (partner, across):
+        pl.semaphore_signal(barrier, inc=1, device_id={"tp": peer}, device_id_type=MESH)
+
+    lane = lax.broadcasted_iota(jnp.int32, (own_rows, LANES), 1)
+    coef = jnp.zeros((own_rows, LANES), F32)
+    for k in range(ids_ref.shape[1]):
+        coef = coef + jnp.where(lane == ids_ref[:, k:k + 1], weight_ref[:, k:k + 1], 0.0)
+    coef_own[...] = coef
+    coef_all[me] = coef
+    tok_all[me] = tok_ref[...]
+    ain_pad[...] = jnp.zeros_like(ain_pad)
+    ain_pad[:, :rank] = ain_ref[0]
+    aout_pad[...] = jnp.zeros_like(aout_pad)
+    aout_pad[:rank, :] = aout_ref[0]
+
+    pl.semaphore_wait(barrier, exp_count + 1)
+
+    def exp_copy(src, dst, send, recv, d):
+        return pltpu.make_async_remote_copy(
+            src_ref=src, dst_ref=dst, send_sem=send.at[d - 1], recv_sem=recv.at[d - 1],
+            device_id={"exp": (me + d) % exp_count}, device_id_type=MESH,
+        )
+
+    tok_copies = [
+        exp_copy(tok_ref, tok_all.at[me], tok_send, tok_recv, d) for d in range(1, exp_count)
+    ]
+    coef_copies = [
+        exp_copy(coef_own, coef_all.at[me], coef_send, coef_recv, d) for d in range(1, exp_count)
+    ]
+    for copy in tok_copies + coef_copies:
+        copy.start()
+
+    def span_cols(j):
+        first, count = spans[j]
+        return pl.ds(first * LANES, (count + (j == last)) * LANES)
+
+    def tp_copy(src, dst, send, recv, j, peer):
+        return pltpu.make_async_remote_copy(
+            src_ref=src, dst_ref=dst, send_sem=send.at[j], recv_sem=recv.at[j],
+            device_id={"tp": peer}, device_id_type=MESH,
+        )
+
+    def s1_copy(j):
+        cols = span_cols(j)
+        return tp_copy(send1.at[:, cols], recv1.at[:, cols], s1_send, s1_recv, j, partner)
+
+    def s2_copy(j):
+        cols = span_cols(j)
+        return tp_copy(send2.at[:, cols], recv2.at[:, cols], s2_send, s2_recv, j, across)
+
+    def hp_copy(j):
+        ref = hid.at[mine, :, span_cols(j)]
+        return tp_copy(ref, ref, hp_send, hp_recv, j, partner)
+
+    def hx_copy(j):
+        ref = hid.at[mine, :, span_cols(j)]
+        return tp_copy(ref, ref, hx_send, hx_recv, j, across)
+
+    def hr_copy(j):
+        ref = hid.at[crossed, :, span_cols(j)]
+        return tp_copy(ref, ref, hr_send, hr_recv, j, partner)
+
+    for copy in tok_copies:
+        copy.wait_recv()
+
+    row = lax.broadcasted_iota(jnp.int32, (LANES, 4 * LANES), 0)
+    col = lax.broadcasted_iota(jnp.int32, (LANES, 4 * LANES), 1)
+    spread = jnp.where(col % (2 * LANES) == 2 * row + col // (2 * LANES), 1.0, 0.0).astype(BF16)
+    ordered = jnp.concatenate([tok_all[b] for b in blocks], axis=0)
+    rows = ordered.shape[0]
+    stacked = jnp.concatenate(
+        [ordered[:, k * LANES:(k + 1) * LANES] for k in range(feat // LANES)], axis=0
+    )
+    wide = jnp.dot(stacked, spread, preferred_element_type=F32).astype(BF16)
+    for k in range(feat // LANES):
+        for p in range(4):
+            for s in range(2):
+                lhs[
+                    (2 * p + s) * own_rows:(2 * p + s + 1) * own_rows,
+                    2 * k * LANES:2 * (k + 1) * LANES,
+                ] = wide[
+                    k * rows + p * own_rows:k * rows + (p + 1) * own_rows,
+                    2 * s * LANES:2 * (s + 1) * LANES,
+                ]
+
+    half = 4 * own_rows
+
+    def store_pair(cols, value):
+        keep1[:, cols] = value[:half]
+        send1[:, cols] = value[half:].astype(BF16)
+
+    def weight_tile(t):
+        return gu.at[t].reshape(2 * feat, LANES)[...]
+
+    def product(j):
+        first, count = spans[j]
+
+        def two(i, carry):
+            t = first + 2 * i
+            gu_copy(t).wait()
+            gu_copy(t + 1).wait()
+            weight = jnp.concatenate([weight_tile(t), weight_tile(t + 1)], axis=1)
+            value = jnp.dot(lhs[...], weight, preferred_element_type=F32)
+            store_pair(pl.ds(pl.multiple_of(t * LANES, LANES), 2 * LANES), value)
+            return carry
+
+        lax.fori_loop(0, count // 2, two, 0)
+        if count % 2:
+            t = first + count - 1
+            gu_copy(t).wait()
+            value = jnp.dot(lhs[...], weight_tile(t), preferred_element_type=F32)
+            store_pair(pl.ds(t * LANES, LANES), value)
+        s1_copy(j).start()
+
+    def rank_product():
+        value = jnp.dot(ordered, ain_pad[...], preferred_element_type=F32)
+        blank = jnp.zeros((own_rows, LANES), F32)
+        parts = []
+        for p in range(4):
+            parts += [value[p * own_rows:(p + 1) * own_rows], blank]
+        store_pair(pl.ds(hidden, LANES), jnp.concatenate(parts, axis=0))
+
+    def reduce_near(j):
+        s1_copy(j).wait_recv()
+        cols = span_cols(j)
+        value = keep1[:, cols] + recv1[:, cols].astype(F32)
+        keep2[:, cols] = value[:2 * own_rows]
+        send2[:, cols] = value[2 * own_rows:].astype(BF16)
+        s2_copy(j).start()
+
+    def activate(j):
+        s2_copy(j).wait_recv()
+        first, count = spans[j]
+        cols = pl.ds(first * LANES, count * LANES)
+        pair = keep2[:, cols] + recv2[:, cols].astype(F32)
+        hid[mine, :, cols] = (jax.nn.silu(pair[:own_rows]) * pair[own_rows:]).astype(BF16)
+        if j == last:
+            cols = pl.ds(hidden, LANES)
+            pair = keep2[:own_rows, cols] + recv2[:own_rows, cols].astype(F32)
+            hid[mine, :, cols] = pair.astype(BF16)
+        hx_copy(j).start()
+        hp_copy(j).start()
+
+    def relay(j):
+        hx_copy(j).wait_recv()
+        hr_copy(j).start()
+
+    def project(j):
+        hp_copy(j).wait_recv()
+        hr_copy(j).wait_recv()
+        down_copy(j).wait()
+        first, count = spans[j]
+        cols = pl.ds(first * LANES, count * LANES)
+        value = jnp.dot(
+            hid[:, :, cols].reshape(rows, count * LANES), down[cols, :],
+            preferred_element_type=F32,
+        )
+        if j == 0:
+            total[...] = value
+        else:
+            total[...] += value
+
+    chunk_count = len(spans)
+    for j in range(chunk_count):
+        product(j)
+        if j == 0:
+            rank_product()
+        else:
+            reduce_near(j - 1)
+        if j >= 4:
+            activate(j - 4)
+    reduce_near(last)
+    done = max(0, chunk_count - 4)
+    for j in range(done, chunk_count):
+        activate(j)
+        if j >= 2:
+            relay(j - 2)
+        if j >= 3:
+            project(j - 3)
+    for j in range(max(0, chunk_count - 2), chunk_count):
+        relay(j)
+    for j in range(max(0, chunk_count - 3), chunk_count):
+        project(j)
+
+    for copy in coef_copies:
+        copy.wait_recv()
+    rank_mid = hid[:, :, pl.ds(hidden, LANES)].reshape(rows, LANES)
+    expert_out = jnp.dot(rank_mid, aout_pad[...], preferred_element_type=F32).astype(BF16)
+    all_coef = coef_all[...].reshape(rows, LANES)
+    wide_lane = lax.broadcasted_iota(jnp.int32, (rows, LANES), 1)
+    column = jnp.sum(jnp.where(wide_lane == me, all_coef, 0.0), axis=1, keepdims=True)
+    part = total[...] + column * expert_out.astype(F32)
+    total[...] = part
+    send_f[...] = part.astype(BF16).reshape(exp_count, own_rows, feat)
+    f_copies = [
+        exp_copy(send_f.at[(me + d) % exp_count], recv_f.at[d - 1], f_send, f_recv, d)
+        for d in range(1, exp_count)
+    ]
+    for copy in f_copies:
+        copy.start()
+    result = total[pl.ds(pl.multiple_of(me * own_rows, own_rows), own_rows), :]
+    for copy, d in zip(f_copies, range(1, exp_count)):
+        copy.wait_recv()
+        result = result + recv_f[d - 1].astype(F32)
+    out_ref[...] = result.astype(out_ref.dtype)
+
+    for copy in tok_copies + coef_copies + f_copies:
+        copy.wait_send()
+    for j in range(chunk_count):
+        for make in (s1_copy, s2_copy, hp_copy, hx_copy, hr_copy):
+            make(j).wait_send()
+
+
+def fused(tokens, gate_up_weight, down_weight, adapter_in, adapter_out, expert_ids, route_weight):
+    exp_count = lax.axis_size("exp")
+    own_rows, feat = tokens.shape
+    hidden = gate_up_weight.shape[2]
+    tiles = hidden // LANES
+    chunk_count = len(chunks_of(tiles))
+    wide = hidden + LANES
+    rows = exp_count * own_rows
+    vmem = functools.partial(pltpu.VMEM)
+    dma = lambda n: pltpu.SemaphoreType.DMA((n,))
+    peers = exp_count - 1
+    in_vmem = pl.BlockSpec(memory_space=pltpu.VMEM)
+    in_place = pl.BlockSpec(memory_space=pl.ANY)
+    return pl.pallas_call(
+        functools.partial(kernel, exp_count),
+        out_shape=jax.ShapeDtypeStruct((own_rows, feat), BF16),
+        in_specs=[in_vmem, in_place, in_place, in_vmem, in_vmem, in_vmem, in_vmem],
+        out_specs=in_vmem,
+        scratch_shapes=[
+            vmem((tiles, feat, 2, LANES), BF16),
+            vmem((hidden, feat), BF16),
+            vmem((exp_count, own_rows, feat), BF16),
+            vmem((exp_count, own_rows, LANES), F32),
+            vmem((own_rows, LANES), F32),
+            vmem((2 * rows, 2 * feat), BF16),
+            vmem((feat, LANES), BF16),
+            vmem((LANES, feat), BF16),
+            vmem((4 * own_rows, wide), F32),
+            vmem((4 * own_rows, wide), BF16),
+            vmem((4 * own_rows, wide), BF16),
+            vmem((2 * own_rows, wide), F32),
+            vmem((2 * own_rows, wide), BF16),
+            vmem((2 * own_rows, wide), BF16),
+            vmem((4, own_rows, wide), BF16),
+            vmem((rows, feat), F32),
+            vmem((exp_count, own_rows, feat), BF16),
+            vmem((peers, own_rows, feat), BF16),
+            dma(tiles), dma(chunk_count),
+            dma(peers), dma(peers), dma(peers), dma(peers),
+            *[dma(chunk_count) for _ in range(10)],
+            dma(peers), dma(peers),
+        ],
+        compiler_params=pltpu.CompilerParams(
+            collective_id=0, has_side_effects=True, vmem_limit_bytes=60 * 2**20
+        ),
+    )(tokens, gate_up_weight, down_weight, adapter_in, adapter_out, expert_ids, route_weight)
+
+
+def plain(tokens, gate_up_weight, down_weight, adapter_in, adapter_out, expert_ids, route_weight):
     exp_count = lax.axis_size("exp")
     own_rows, feat_width = tokens.shape
     all_tokens = lax.all_gather(tokens, "exp", axis=0, tiled=True)
@@ -71,6 +398,20 @@
     return (base_out + adapter_sum).astype(jnp.bfloat16)
 
 
+def local(tokens, gate_up_weight, *rest):
+    own_rows, feat = tokens.shape
+    fits = (
+        lax.axis_size("tp") == 4
+        and lax.axis_size("exp") == 4
+        and rest[1].shape[0] == 1
+        and rest[1].shape[2] <= LANES
+        and own_rows % 16 == 0
+        and feat % LANES == 0
+        and gate_up_weight.shape[2] % LANES == 0
+    )
+    return (fused if fits else plain)(tokens, gate_up_weight, *rest)
+
+
 def solution(mesh):
     in_specs = (
         P(("grp", "exp"), "tp"),

time: 106 us -> 44.7 us (0.42)
  Pallas kernels: 0 us -> 38.7 us
  blocking collectives: 34.4 us -> 0 us
  waiting for transfers between devices: 25.7 us -> 0 us
  between operations: 13.5 us -> 0.01 us
  matrix products: 12.4 us -> 0 us
  starting transfers between devices: 8.16 us -> 0 us
  local copies, waits for them, and re-layouts: 10.1 us -> 5.61 us
  other arithmetic: 1.49 us -> 0 us
    pallas_call x0 -> x1, Pallas kernels: none -> 38.7 us  [fused(): pl.pallas_call(functools.partial(kernel, exp_count), out_shape=jax.ShapeD...]
    all_gather x2 -> x0, blocking collectives: 23.2 us -> none  [the longest x1 15.4 us: local(): all_tokens = lax.all_gather(tokens, 'exp', axis=0, tiled=True)]
    reduce_scatter x2 -> x0, waiting for transfers between devices: 20 us -> none  [the longest x1 20 us: local(): lax.psum_scatter(jnp.dot(hidden, down_weight, preferred_element_type=jnp....]
    dot_general x6 -> x0, matrix products: 12.4 us -> none  [the longest x1 5.47 us: local(): jnp.dot(hidden, down_weight, preferred_element_type=jnp.float32)]
    psum x1 -> x0, blocking collectives: 11.2 us -> none  [local(): rank_mid = lax.psum(rank_partial, 'tp').astype(jnp.bfloat16)]
    all_to_all x2 -> x0, starting transfers between devices: 8.11 us -> none  [the longest x1 4.8 us: local(): lax.all_to_all(outgoing, 'exp', split_axis=0, concat_axis=0, tiled=True)]
    all_to_all x2 -> x0, waiting for transfers between devices: 5.72 us -> none  [the longest x1 5.71 us: local(): lax.all_to_all(outgoing, 'exp', split_axis=0, concat_axis=0, tiled=True)]
    unnamed x12 -> x4, local copies, waits for them, and re-layouts: 9.81 us -> 5.61 us
  transfers between devices with their start and end apart: 4 -> 0, of which waited for: 2 -> 0; matrix products, arithmetic and copies ran while one was open for 9% -> 0% of each run, Pallas kernels for 0% -> 0%
where the time goes in v1:
time: 44.7 us; the launch traced here: 44.4 us
  Pallas kernels  38.7 us (87%)
  local copies, waits for them, and re-layouts  5.61 us (13%)
    pallas_call x1, Pallas kernels, fused(): pl.pallas_call(functools.partial(kernel, exp_count), out_shape=jax.ShapeD...  38.7 us
    unnamed x4, local copies, waits for them, and re-layouts  5.61 us

profile of v1, /device:TPU:0, one launch (start us, length us, event | category | flops | bytes accessed | tf_op | source)
XLA Modules:
  0.0 44.4 jit_solution(16144486116273547817)
XLA Ops:
  0.0 1.4 %copy.9.ids_ref = s32[16,2]{1,0:T(8,128)} copy(s32[16,2]{0,1:T(2,128)} %param.12) | data formatting | bytes 256 | tf_op args[5]
  1.4 1.3 %copy.10.weight_ref = f32[16,2]{1,0:T(8,128)} copy(f32[16,2]{0,1:T(2,128)} %param.13) | data formatting | bytes 256 | tf_op args[6]
  2.7 1.6 %copy.8.ain_ref = bf16[1,896,16]{2,1,0:T(8,128)(2,1)} copy(bf16[1,896,16]{1,2,0:T(8,128)(2,1)} %param.10) | data formatting | bytes 57344 | tf_op args[3]
  4.3 38.7 %shard_map.73 = bf16[16,896]{1,0:T(8,128)(2,1)} custom-call(bf16[16,896]{1,0:T(8,128)(2,1)} %tok_ref.1, bf16[896,2,4736]{2,1,0:T(2,128)(2,1)} %gu_ref.1, bf16[4736,896]{1,0:T(8,128)(2,1)} %down_ref.1, bf16[1,896,16]{2,1,0:T(8,128)(2,1)} %copy.8.ain_ref, bf16[1,16,896]{2,1,0:T(8,128)(2,1)} %aout_ref.1, s32[16,2]{1,0:T(8,128)} %copy.9.ids_ref, ...), custom_call_target="tpu_custom_call" | custom-call | tf_op jit(solution)/shard_map/pallas_call | solution.py:299
  43.0 1.4 %copy.12 = bf16[16,896]{1,0:T(8,128)(2,1)} copy(bf16[16,896]{1,0:T(8,128)(2,1)} %shard_map.73) | data formatting | bytes 57344

commit v2 on v1

--- a/solution.py
+++ b/solution.py
@@ -33,7 +33,7 @@
     tp = lax.axis_index("tp")
     own_rows, feat = tok_ref.shape
     hidden = gu_ref.shape[2]
-    rank = ain_ref.shape[2]
+    rank = ain_ref.shape[1]
     tiles = hidden // LANES
     spans = chunks_of(tiles)
     last = len(spans) - 1
@@ -74,14 +74,22 @@
         pl.semaphore_signal(barrier, inc=1, device_id={"tp": peer}, device_id_type=MESH)
 
     lane = lax.broadcasted_iota(jnp.int32, (own_rows, LANES), 1)
+    diagonal = lax.broadcasted_iota(
+        jnp.int32, (own_rows, own_rows), 0
+    ) == lax.broadcasted_iota(jnp.int32, (own_rows, own_rows), 1)
+
+    def column_of(line):
+        return jnp.sum(jnp.where(diagonal, line, 0.0), axis=1, keepdims=True)
+
     coef = jnp.zeros((own_rows, LANES), F32)
-    for k in range(ids_ref.shape[1]):
-        coef = coef + jnp.where(lane == ids_ref[:, k:k + 1], weight_ref[:, k:k + 1], 0.0)
+    for k in range(ids_ref.shape[0]):
+        named = column_of(ids_ref[k:k + 1, :].astype(F32)).astype(jnp.int32)
+        coef = coef + jnp.where(lane == named, column_of(weight_ref[k:k + 1, :]), 0.0)
     coef_own[...] = coef
     coef_all[me] = coef
     tok_all[me] = tok_ref[...]
     ain_pad[...] = jnp.zeros_like(ain_pad)
-    ain_pad[:, :rank] = ain_ref[0]
+    ain_pad[:rank, :] = ain_ref[0]
     aout_pad[...] = jnp.zeros_like(aout_pad)
     aout_pad[:rank, :] = aout_ref[0]
 
@@ -185,7 +193,9 @@
         s1_copy(j).start()
 
     def rank_product():
-        value = jnp.dot(ordered, ain_pad[...], preferred_element_type=F32)
+        value = lax.dot_general(
+            ordered, ain_pad[...], (((1,), (1,)), ((), ())), preferred_element_type=F32
+        )
         blank = jnp.zeros((own_rows, LANES), F32)
         parts = []
         for p in range(4):
@@ -308,7 +318,7 @@
             vmem((exp_count, own_rows, LANES), F32),
             vmem((own_rows, LANES), F32),
             vmem((2 * rows, 2 * feat), BF16),
-            vmem((feat, LANES), BF16),
+            vmem((LANES, feat), BF16),
             vmem((LANES, feat), BF16),
             vmem((4 * own_rows, wide), F32),
             vmem((4 * own_rows, wide), BF16),
@@ -328,7 +338,10 @@
         compiler_params=pltpu.CompilerParams(
             collective_id=0, has_side_effects=True, vmem_limit_bytes=60 * 2**20
         ),
-    )(tokens, gate_up_weight, down_weight, adapter_in, adapter_out, expert_ids, route_weight)
+    )(
+        tokens, gate_up_weight, down_weight, jnp.swapaxes(adapter_in, 1, 2), adapter_out,
+        expert_ids.T, route_weight.T,
+    )
 
 
 def plain(tokens, gate_up_weight, down_weight, adapter_in, adapter_out, expert_ids, route_weight):

time: 44.7 us -> 40.2 us (0.90)
  local copies, waits for them, and re-layouts: 5.61 us -> 1.36 us
    unnamed x4 -> x1, local copies, waits for them, and re-layouts: 5.61 us -> 1.36 us
where the time goes in v2:
time: 40.2 us; the launch traced here: 40 us
  Pallas kernels  38.6 us (96%)
  local copies, waits for them, and re-layouts  1.36 us (3%)
    pallas_call x1, Pallas kernels, fused(): pl.pallas_call(functools.partial(kernel, exp_count), out_shape=jax.ShapeD...  38.6 us
    unnamed x1, local copies, waits for them, and re-layouts  1.36 us

profile of v2, /device:TPU:0, one launch (start us, length us, event | category | flops | bytes accessed | tf_op | source)
XLA Modules:
  0.0 40.0 jit_solution(3656800096092567917)
XLA Ops:
  0.0 38.6 %shard_map.73 = bf16[16,896]{1,0:T(8,128)(2,1)} custom-call(bf16[16,896]{1,0:T(8,128)(2,1)} %tok_ref.1, bf16[896,2,4736]{2,1,0:T(2,128)(2,1)} %gu_ref.1, bf16[4736,896]{1,0:T(8,128)(2,1)} %down_ref.1, bf16[1,16,896]{2,1,0:T(8,128)(2,1)} %bitcast.3, bf16[1,16,896]{2,1,0:T(8,128)(2,1)} %aout_ref.1, s32[2,16]{1,0:T(2,128)} %bitcast.4, f32[2,16]{1,0:T(2,128)} %bitcast.5), custom_call_target="tpu_custom_call" | custom-call | tf_op jit(solution)/shard_map/pallas_call | solution.py:309
  38.6 1.4 %copy.9 = bf16[16,896]{1,0:T(8,128)(2,1)} copy(bf16[16,896]{1,0:T(8,128)(2,1)} %shard_map.73) | data formatting | bytes 57344

commit v3 on v2

--- a/solution.py
+++ b/solution.py
@@ -8,6 +8,7 @@
 
 LANES = 128
 CHUNK_TILES = 8
+STEP_TILES = 4
 MESH = pl.DeviceIdType.MESH
 BF16, F32 = jnp.bfloat16, jnp.float32
 
@@ -48,9 +49,11 @@
     ]
     mine, crossed = blocks[0], blocks[1]
 
+    gu_flat = gu_ref.reshape(2 * feat, hidden)
+
     def gu_copy(t):
         cols = pl.ds(pl.multiple_of(t * LANES, LANES), LANES)
-        return pltpu.make_async_copy(gu_ref.at[:, :, cols], gu.at[t], gu_sem.at[t])
+        return pltpu.make_async_copy(gu_flat.at[:, cols], gu.at[t], gu_sem.at[t])
 
     def down_copy(j):
         first, count = spans[j]
@@ -112,7 +115,9 @@
 
     def span_cols(j):
         first, count = spans[j]
-        return pl.ds(first * LANES, (count + (j == last)) * LANES)
+        if j == 0:
+            return pl.ds(0, (count + 1) * LANES)
+        return pl.ds((first + 1) * LANES, count * LANES)
 
     def tp_copy(src, dst, send, recv, j, peer):
         return pltpu.make_async_remote_copy(
@@ -169,27 +174,23 @@
         keep1[:, cols] = value[:half]
         send1[:, cols] = value[half:].astype(BF16)
 
-    def weight_tile(t):
-        return gu.at[t].reshape(2 * feat, LANES)[...]
-
     def product(j):
         first, count = spans[j]
 
-        def two(i, carry):
-            t = first + 2 * i
-            gu_copy(t).wait()
-            gu_copy(t + 1).wait()
-            weight = jnp.concatenate([weight_tile(t), weight_tile(t + 1)], axis=1)
+        def several(t, width):
+            for i in range(width):
+                gu_copy(t + i).wait()
+            weight = jnp.concatenate([gu[t + i] for i in range(width)], axis=1)
             value = jnp.dot(lhs[...], weight, preferred_element_type=F32)
-            store_pair(pl.ds(pl.multiple_of(t * LANES, LANES), 2 * LANES), value)
+            store_pair(pl.ds(pl.multiple_of((t + 1) * LANES, LANES), width * LANES), value)
+
+        def step(i, carry):
+            several(first + STEP_TILES * i, STEP_TILES)
             return carry
 
-        lax.fori_loop(0, count // 2, two, 0)
-        if count % 2:
-            t = first + count - 1
-            gu_copy(t).wait()
-            value = jnp.dot(lhs[...], weight_tile(t), preferred_element_type=F32)
-            store_pair(pl.ds(t * LANES, LANES), value)
+        lax.fori_loop(0, count // STEP_TILES, step, 0)
+        if count % STEP_TILES:
+            several(first + count - count % STEP_TILES, count % STEP_TILES)
         s1_copy(j).start()
 
     def rank_product():
@@ -200,7 +201,7 @@
         parts = []
         for p in range(4):
             parts += [value[p * own_rows:(p + 1) * own_rows], blank]
-        store_pair(pl.ds(hidden, LANES), jnp.concatenate(parts, axis=0))
+        store_pair(pl.ds(0, LANES), jnp.concatenate(parts, axis=0))
 
     def reduce_near(j):
         s1_copy(j).wait_recv()
@@ -213,11 +214,11 @@
     def activate(j):
         s2_copy(j).wait_recv()
         first, count = spans[j]
-        cols = pl.ds(first * LANES, count * LANES)
+        cols = pl.ds((first + 1) * LANES, count * LANES)
         pair = keep2[:, cols] + recv2[:, cols].astype(F32)
         hid[mine, :, cols] = (jax.nn.silu(pair[:own_rows]) * pair[own_rows:]).astype(BF16)
-        if j == last:
-            cols = pl.ds(hidden, LANES)
+        if j == 0:
+            cols = pl.ds(0, LANES)
             pair = keep2[:own_rows, cols] + recv2[:own_rows, cols].astype(F32)
             hid[mine, :, cols] = pair.astype(BF16)
         hx_copy(j).start()
@@ -226,28 +227,39 @@
     def relay(j):
         hx_copy(j).wait_recv()
         hr_copy(j).start()
+
+    def adapter_part():
+        for copy in coef_copies:
+            copy.wait_recv()
+        rank_mid = hid[:, :, pl.ds(0, LANES)].reshape(rows, LANES)
+        expert_out = jnp.dot(rank_mid, aout_pad[...], preferred_element_type=F32).astype(BF16)
+        all_coef = coef_all[...].reshape(rows, LANES)
+        wide_lane = lax.broadcasted_iota(jnp.int32, (rows, LANES), 1)
+        column = jnp.sum(jnp.where(wide_lane == me, all_coef, 0.0), axis=1, keepdims=True)
+        return column * expert_out.astype(F32)
 
     def project(j):
         hp_copy(j).wait_recv()
         hr_copy(j).wait_recv()
         down_copy(j).wait()
         first, count = spans[j]
-        cols = pl.ds(first * LANES, count * LANES)
+        cols = pl.ds((first + 1) * LANES, count * LANES)
         value = jnp.dot(
-            hid[:, :, cols].reshape(rows, count * LANES), down[cols, :],
+            hid[:, :, cols].reshape(rows, count * LANES),
+            down[pl.ds(first * LANES, count * LANES), :],
             preferred_element_type=F32,
         )
         if j == 0:
-            total[...] = value
+            total[...] = value + adapter_part()
         else:
             total[...] += value
 
     chunk_count = len(spans)
     for j in range(chunk_count):
-        product(j)
         if j == 0:
             rank_product()
-        else:
+        product(j)
+        if j > 0:
             reduce_near(j - 1)
         if j >= 4:
             activate(j - 4)
@@ -264,15 +276,7 @@
     for j in range(max(0, chunk_count - 3), chunk_count):
         project(j)
 
-    for copy in coef_copies:
-        copy.wait_recv()
-    rank_mid = hid[:, :, pl.ds(hidden, LANES)].reshape(rows, LANES)
-    expert_out = jnp.dot(rank_mid, aout_pad[...], preferred_element_type=F32).astype(BF16)
-    all_coef = coef_all[...].reshape(rows, LANES)
-    wide_lane = lax.broadcasted_iota(jnp.int32, (rows, LANES), 1)
-    column = jnp.sum(jnp.where(wide_lane == me, all_coef, 0.0), axis=1, keepdims=True)
-    part = total[...] + column * expert_out.astype(F32)
-    total[...] = part
+    part = total[...]
     send_f[...] = part.astype(BF16).reshape(exp_count, own_rows, feat)
     f_copies = [
         exp_copy(send_f.at[(me + d) % exp_count], recv_f.at[d - 1], f_send, f_recv, d)
@@ -312,7 +316,7 @@
         in_specs=[in_vmem, in_place, in_place, in_vmem, in_vmem, in_vmem, in_vmem],
         out_specs=in_vmem,
         scratch_shapes=[
-            vmem((tiles, feat, 2, LANES), BF16),
+            vmem((tiles, 2 * feat, LANES), BF16),
             vmem((hidden, feat), BF16),
             vmem((exp_count, own_rows, feat), BF16),
             vmem((exp_count, own_rows, LANES), F32),

time: 40.2 us -> 35.4 us (0.88)
  Pallas kernels: 38.6 us -> 33.8 us
    pallas_call x1, Pallas kernels: 38.6 us -> 33.8 us  [fused(): pl.pallas_call(functools.partial(kernel, exp_count), out_shape=jax.ShapeD...]
where the time goes in v3:
time: 35.4 us; the launch traced here: 35.2 us
  Pallas kernels  33.8 us (95%)
  local copies, waits for them, and re-layouts  1.36 us (4%)
    pallas_call x1, Pallas kernels, fused(): pl.pallas_call(functools.partial(kernel, exp_count), out_shape=jax.ShapeD...  33.8 us
    unnamed x1, local copies, waits for them, and re-layouts  1.36 us

profile of v3, /device:TPU:0, one launch (start us, length us, event | category | flops | bytes accessed | tf_op | source)
XLA Modules:
  0.0 35.2 jit_solution(14185919480001617151)
XLA Ops:
  0.0 33.8 %shard_map.73 = bf16[16,896]{1,0:T(8,128)(2,1)} custom-call(bf16[16,896]{1,0:T(8,128)(2,1)} %tok_ref.1, bf16[896,2,4736]{2,1,0:T(2,128)(2,1)} %gu_ref.1, bf16[4736,896]{1,0:T(8,128)(2,1)} %down_ref.1, bf16[1,16,896]{2,1,0:T(8,128)(2,1)} %bitcast.3, bf16[1,16,896]{2,1,0:T(8,128)(2,1)} %aout_ref.1, s32[2,16]{1,0:T(2,128)} %bitcast.4, f32[2,16]{1,0:T(2,128)} %bitcast.5), custom_call_target="tpu_custom_call" | custom-call | tf_op jit(solution)/shard_map/pallas_call | solution.py:313
  33.8 1.4 %copy.9 = bf16[16,896]{1,0:T(8,128)(2,1)} copy(bf16[16,896]{1,0:T(8,128)(2,1)} %shard_map.73) | data formatting | bytes 57344

commit v4 on v3

--- a/solution.py
+++ b/solution.py
@@ -7,8 +7,9 @@
 from jax.sharding import PartitionSpec as P
 
 LANES = 128
-CHUNK_TILES = 8
-STEP_TILES = 4
+CHUNK_TILES = 6
+STEP_TILES = 6
+RELAY_LAG = 6
 MESH = pl.DeviceIdType.MESH
 BF16, F32 = jnp.bfloat16, jnp.float32
 
@@ -37,7 +38,6 @@
     rank = ain_ref.shape[1]
     tiles = hidden // LANES
     spans = chunks_of(tiles)
-    last = len(spans) - 1
     core, side = tp % 2, tp // 2
     partner = side * 2 + (1 - core)
     across = (1 - side) * 2 + core
@@ -255,26 +255,14 @@
             total[...] += value
 
     chunk_count = len(spans)
-    for j in range(chunk_count):
-        if j == 0:
-            rank_product()
-        product(j)
-        if j > 0:
-            reduce_near(j - 1)
-        if j >= 4:
-            activate(j - 4)
-    reduce_near(last)
-    done = max(0, chunk_count - 4)
-    for j in range(done, chunk_count):
-        activate(j)
-        if j >= 2:
-            relay(j - 2)
-        if j >= 3:
-            project(j - 3)
-    for j in range(max(0, chunk_count - 2), chunk_count):
-        relay(j)
-    for j in range(max(0, chunk_count - 3), chunk_count):
-        project(j)
+    stages = (
+        (product, 0), (reduce_near, 1), (activate, 4), (relay, RELAY_LAG), (project, RELAY_LAG + 1),
+    )
+    rank_product()
+    for step in range(chunk_count + RELAY_LAG + 1):
+        for stage, lag in stages:
+            if 0 <= step - lag < chunk_count:
+                stage(step - lag)
 
     part = total[...]
     send_f[...] = part.astype(BF16).reshape(exp_count, own_rows, feat)

time: 35.4 us -> 34.9 us (0.986)
  Pallas kernels: 33.8 us -> 33.3 us
    pallas_call x1, Pallas kernels: 33.8 us -> 33.3 us  [fused(): pl.pallas_call(functools.partial(kernel, exp_count), out_shape=jax.ShapeD...]
where the time goes in v4:
time: 34.9 us; the launch traced here: 34.7 us
  Pallas kernels  33.3 us (95%)
  local copies, waits for them, and re-layouts  1.36 us (4%)
    pallas_call x1, Pallas kernels, fused(): pl.pallas_call(functools.partial(kernel, exp_count), out_shape=jax.ShapeD...  33.3 us
    unnamed x1, local copies, waits for them, and re-layouts  1.36 us

profile of v4, /device:TPU:0, one launch (start us, length us, event | category | flops | bytes accessed | tf_op | source)
XLA Modules:
  0.0 34.7 jit_solution(1198749876875907179)
XLA Ops:
  0.0 33.3 %shard_map.73 = bf16[16,896]{1,0:T(8,128)(2,1)} custom-call(bf16[16,896]{1,0:T(8,128)(2,1)} %tok_ref.1, bf16[896,2,4736]{2,1,0:T(2,128)(2,1)} %gu_ref.1, bf16[4736,896]{1,0:T(8,128)(2,1)} %down_ref.1, bf16[1,16,896]{2,1,0:T(8,128)(2,1)} %bitcast.3, bf16[1,16,896]{2,1,0:T(8,128)(2,1)} %aout_ref.1, s32[2,16]{1,0:T(2,128)} %bitcast.4, f32[2,16]{1,0:T(2,128)} %bitcast.5), custom_call_target="tpu_custom_call" | custom-call | tf_op jit(solution)/shard_map/pallas_call | solution.py:301
  33.3 1.4 %copy.9 = bf16[16,896]{1,0:T(8,128)(2,1)} copy(bf16[16,896]{1,0:T(8,128)(2,1)} %shard_map.73) | data formatting | bytes 57344
